TPU v7x, 32 devices: a whole 2x2x4 slice. The times are simulated.
32 devices in a mesh: dp: 4 (over x, core), fsdp: 4 (over z), mp: 2 (over y).
Axes of the slice: x: 2, y: 2, z: 4, core: 2. Of those that a mesh axis runs over, the one named last changes fastest.
Arguments:
- tokens_in: bfloat16 [4096, 3072], P(('dp', 'fsdp', 'mp')), may hold values from -40 to 40
- segment_ids: int32 [4096], P(('dp', 'fsdp', 'mp')), may hold values from 0 to 31, never falling along the last dimension, each value on 1 to 512 neighbouring positions
- target_ids: int32 [4096], P(('dp', 'fsdp', 'mp')), may hold values from 0 to 8191
- old_weights: bfloat16 [4, 3072, 2048], P(None, ('dp', 'fsdp', 'mp'))
- old_first: float32 [4, 3072, 2048], P(None, ('dp', 'fsdp', 'mp')), may hold values from -6 to 6
- old_second: float32 [4, 3072, 2048], P(None, ('dp', 'fsdp', 'mp')), may hold values from 0.01 to 4
- old_block: int32 [32], P(('dp', 'fsdp', 'mp')), may hold values from 0 to 31, each once
- new_residue: int32 [4], P('dp'), may hold values from 0 to 3, each once
- norm_gain: float32 [3072], replicated, may hold values from 0.5 to 1.5
- head_weight: bfloat16 [3072, 8192], P(None, ('fsdp', 'mp'))
Outputs:
- new_weights: bfloat16 [4, 3072, 2048], P(None, 'dp', ('fsdp', 'mp'))
- new_first: float32 [4, 3072, 2048], P(None, 'dp', ('fsdp', 'mp'))
- new_second: float32 [4, 3072, 2048], P(None, 'dp', ('fsdp', 'mp'))
- loss: float32 [4096], P(('dp', 'fsdp', 'mp'))
Inputs may be any that keep to these rules, and one draw needn't show every extreme that they name: `old_block`: a permutation of the old layout's row blocks. `new_residue`: a permutation; index i of dp holds the rows whose number modulo 4 is new_residue[i], in rising order. `segment_ids`: never falling along the tokens.
All inputs are finite; a program needn't handle non-finite values.
Results may differ from a plain program's by a relative error of at most 0.0075.
Values may be sent and summed in bfloat16 or wider, within the bound.
A program may use at most 192 MiB of HBM per device.

v0:
```python
import math
import jax
import jax.numpy as jnp
from jax import lax
from jax.sharding import PartitionSpec as P

HD = 128


def inverse_of(table):
    total_count = table.shape[0]
    places = jnp.arange(total_count, dtype=jnp.int32)
    return jnp.sum(jnp.where(table[None, :] == places[:, None], places[None, :], 0), axis=1)


def pack_rows(stored, residues, fm_count):
    matrices, row_count, columns = stored.shape
    dp_count = residues.shape[0]
    split_rows = stored.reshape(
        matrices, row_count // dp_count, dp_count, fm_count, columns // fm_count
    )
    chosen = jnp.take(split_rows, residues, axis=2, mode="clip")
    return chosen.transpose(2, 3, 0, 1, 4).reshape(
        dp_count * fm_count, matrices, row_count // dp_count, columns // fm_count
    )


def unpack_rows(received, holder):
    ordered = jnp.take(received, holder, axis=0, mode="clip")
    devices, matrices, pair_rows, group_cols = ordered.shape
    return ordered.transpose(1, 0, 2, 3).reshape(matrices, devices * pair_rows, group_cols)


def norm_rows(hidden, norm_gain):
    scale = lax.rsqrt(jnp.mean(hidden * hidden, axis=1, keepdims=True) + 1e-05)
    return (hidden * scale * norm_gain).astype(jnp.bfloat16)


FLAGS = dict(tail="a2a", first="before_rs", second="free", tokens="first")


def share_tables(segment_ids, target_ids, old_block, new_residue):
    axes = ("dp", "fsdp", "mp")
    own = jnp.concatenate([segment_ids, target_ids, old_block, new_residue])
    rows = jnp.broadcast_to(own[None, None], (lax.axis_size(axes), 1, own.shape[0]))
    rows = lax.all_to_all(rows, axes, split_axis=0, concat_axis=0, tiled=True)[:, 0]
    count = segment_ids.shape[0]
    fm_count = lax.axis_size(("fsdp", "mp"))
    here = lax.dynamic_slice_in_dim(rows, lax.axis_index("dp") * fm_count, fm_count)
    segments = here[:, :count].reshape(-1)
    targets = here[:, count : 2 * count].reshape(-1)
    return (segments, targets, rows[:, 2 * count], rows[::fm_count, 2 * count + 1])


def joint_loss(row_top, row_total, picked):
    axes = ("fsdp", "mp")
    fm_count = lax.axis_size(axes)
    parts = jnp.stack([row_top, row_total, picked])
    own_count = parts.shape[1] // fm_count
    if FLAGS["tail"] == "a2a":
        parts = parts.reshape(3, fm_count, own_count).transpose(1, 0, 2)
        parts = lax.all_to_all(parts, axes, split_axis=0, concat_axis=0, tiled=True)
    else:
        place = lax.axis_index(axes)
        rows = jnp.zeros((fm_count,) + parts.shape, jnp.float32)
        rows = lax.psum(lax.dynamic_update_slice(rows, parts[None], (place, 0, 0)), axes)
        parts = lax.dynamic_slice_in_dim(rows, place * own_count, own_count, axis=2)
    tops, totals, targets = (parts[:, 0], parts[:, 1], parts[:, 2])
    joint_max = jnp.max(tops, axis=0)
    joint_total = jnp.sum(totals * jnp.exp(tops - joint_max[None]), axis=0)
    return joint_max + jnp.log(joint_total) - jnp.sum(targets, axis=0)


def body(
    tokens_in,
    segment_ids,
    target_ids,
    old_weights,
    old_first,
    old_second,
    old_block,
    new_residue,
    norm_gain,
    head_weight,
):
    dp_count = lax.axis_size("dp")
    fm_count = lax.axis_size(("fsdp", "mp"))
    everyone = ("dp", "fsdp", "mp")
    columns = old_weights.shape[2]
    group_cols = columns // fm_count
    model_width = tokens_in.shape[1]
    new_rows = model_width // dp_count
    segments, targets, table_all, residues = share_tables(
        segment_ids, target_ids, old_block, new_residue
    )
    holder = inverse_of(table_all)
    inverse_res = inverse_of(residues)
    feature_ids = (
        residues[:, None] + dp_count * jnp.arange(new_rows, dtype=jnp.int32)[None]
    ).reshape(-1)
    logical_ids = (
        jnp.arange(new_rows, dtype=jnp.int32)[:, None] + new_rows * inverse_res[None]
    ).reshape(-1)
    own_picked = jnp.take(tokens_in, feature_ids, axis=1, mode="clip")
    picked_cols = lax.all_gather(own_picked, ("fsdp", "mp"), axis=0, tiled=True)
    seq_len = picked_cols.shape[0]
    weights_sent = pack_rows(old_weights, residues, fm_count)
    weights_got = lax.all_to_all(weights_sent, everyone, split_axis=0, concat_axis=0, tiled=True)
    first_sent = pack_rows(old_first, residues, fm_count)
    second_sent = pack_rows(old_second, residues, fm_count)
    if FLAGS["first"] != "free":
        weights_got, first_sent, second_sent = lax.optimization_barrier(
            (weights_got, first_sent, second_sent)
        )
    new_weights = unpack_rows(weights_got, holder)
    projections = new_weights[:3]
    if FLAGS.get("tokens") == "first":
        picked_cols, projections, first_sent = lax.optimization_barrier(
            (picked_cols, projections, first_sent)
        )
    first_got = lax.all_to_all(first_sent, everyone, split_axis=0, concat_axis=0, tiled=True)
    piece = lax.all_gather(projections, "dp", axis=1, tiled=True)
    projected = jnp.einsum("sr,mrc->msc", picked_cols, piece, preferred_element_type=jnp.float32)
    heads = group_cols // HD
    queries = projected[0].astype(jnp.bfloat16).reshape(seq_len, heads, HD)
    keys_all = projected[1].astype(jnp.bfloat16).reshape(seq_len, heads, HD)
    values_all = projected[2].astype(jnp.bfloat16).reshape(seq_len, heads, HD)
    positions_all = jnp.arange(seq_len, dtype=jnp.int32)
    allowed = (positions_all[:, None] >= positions_all[None, :]) & (
        segments[:, None] == segments[None, :]
    )
    scores = jnp.einsum("shd,thd->hst", queries, keys_all, preferred_element_type=jnp.float32) * (
        1.0 / math.sqrt(HD)
    )
    scores = jnp.where(allowed[None], scores, -1e30)
    row_max = jnp.max(scores, axis=2, keepdims=True)
    expo = jnp.where(allowed[None], jnp.exp(scores - row_max), 0.0)
    soft = (expo / jnp.sum(expo, axis=2, keepdims=True)).astype(jnp.bfloat16)
    attended = jnp.einsum("hst,thd->shd", soft, values_all, preferred_element_type=jnp.float32)
    attended = attended.astype(jnp.bfloat16).reshape(seq_len, group_cols)
    shuffled = jnp.einsum(
        "sc,rc->sr",
        attended,
        lax.all_gather(new_weights[3], "dp", axis=0, tiled=True),
        preferred_element_type=jnp.float32,
    )
    partial_value = shuffled.astype(jnp.bfloat16)
    if FLAGS["first"] == "rs_first":
        partial_value, second_sent = lax.optimization_barrier((partial_value, second_sent))
    if FLAGS["first"] == "before_rs":
        partial_value, first_got, second_sent = lax.optimization_barrier(
            (partial_value, first_got, second_sent)
        )
    second_got = lax.all_to_all(second_sent, everyone, split_axis=0, concat_axis=0, tiled=True)
    own_sum = lax.psum_scatter(partial_value, ("fsdp", "mp"), scatter_dimension=0, tiled=True)
    own_sum = jnp.take(own_sum, logical_ids, axis=1, mode="clip").astype(jnp.float32)
    own_normed = norm_rows(tokens_in.astype(jnp.float32) + own_sum, norm_gain)
    if FLAGS["second"] == "before_ag":
        own_normed, second_got = lax.optimization_barrier((own_normed, second_got))
    new_first = unpack_rows(first_got, holder)
    new_second = unpack_rows(second_got, holder)
    normed = lax.all_gather(own_normed, ("fsdp", "mp"), axis=0, tiled=True)
    logits = jnp.dot(normed, head_weight, preferred_element_type=jnp.float32)
    vocab_dev = logits.shape[1]
    offset = lax.axis_index(("fsdp", "mp")) * vocab_dev
    row_top = jnp.max(logits, axis=1)
    row_total = jnp.sum(jnp.exp(logits - row_top[:, None]), axis=1)
    vocab_ids = jnp.arange(vocab_dev, dtype=jnp.int32) + offset
    picked = jnp.sum(jnp.where(vocab_ids[None, :] == targets[:, None], logits, 0.0), axis=1)
    loss = joint_loss(row_top, row_total, picked)
    return (new_weights, new_first, new_second, loss)


def solution(mesh):
    placed = (
        P(("dp", "fsdp", "mp"), None),
        P(("dp", "fsdp", "mp")),
        P(("dp", "fsdp", "mp")),
        P(None, ("dp", "fsdp", "mp"), None),
        P(None, ("dp", "fsdp", "mp"), None),
        P(None, ("dp", "fsdp", "mp"), None),
        P(("dp", "fsdp", "mp")),
        P("dp"),
        P(),
        P(None, ("fsdp", "mp")),
    )
    return jax.shard_map(
        body,
        mesh=mesh,
        in_specs=placed,
        out_specs=(
            P(None, "dp", ("fsdp", "mp")),
            P(None, "dp", ("fsdp", "mp")),
            P(None, "dp", ("fsdp", "mp")),
            P(("dp", "fsdp", "mp")),
        ),
        check_vma=False,
    )
```

profile of v0, /device:TPU:0, one launch (start us, length us, event | category | flops | bytes accessed | tf_op | source)
XLA Modules:
  0.0 589.0 jit_solution(5896758327097351042)
XLA Ops:
  8.5 0.7 pad_add_fusion
  9.2 0.6 broadcast_in_dim.85
  9.9 7.3 %all-to-all-start = ((s32[32,1,258]{2,1,0:T(1,128)}), s32[32,1,258]{2,1,0:T(1,128)S(1)}, u32[]{:S(2)}, u32[]{:S(2)}) async-start(s32[32,1,258]{2,1,0:T(1,128)} %broadcast_in_dim.85), calls=%async_computation | async-start | bytes 98304 | tf_op jit(solution)/shard_map/all_to_all | solution.py:46
  17.2 0.0 all-gather.12.cloned.1.call-start
  17.2 1.5 copy.84
  18.8 5.7 all-to-all-done
  24.4 0.1 slice.43
  24.5 0.1 reduce.2
  24.6 0.1 broadcast_add_fusion
  24.7 11.4 %gather_fusion.4 = bf16[3072,128]{1,0:T(8,128)(2,1)} fusion(bf16[128,3072]{0,1:T(8,128)(2,1)S(1)} %copy.84, s32[3072]{0:T(1024)S(1)} %broadcast_clamp_fusion.1), kind=kCustom, calls=%fused_computation.4 | custom fusion | bytes 1585152 | tf_op jit(solution)/shard_map/jit(_take)/gather | solution.py:104
  36.2 1.9 copy.104
  38.1 1.9 gather_fusion
  40.0 3.1 copy.80
  43.2 2.7 all-to-all-start.1
  45.9 0.0 all-gather.6.cloned.1.call-start
  45.9 5.1 copy.105
  51.0 3.1 copy.106
  54.2 4.3 gather_fusion.1
  58.5 4.5 copy.81
  63.0 4.4 gather_fusion.2
  67.4 4.6 copy.82
  72.0 0.1 slice_reduce_fusion
  72.1 0.1 select_reduce_fusion.1
  72.2 34.0 %all-to-all-done.1 = bf16[32,4,24,256]{3,2,1,0:T(8,128)(2,1)S(1)} async-done(((bf16[32,4,24,256]{3,2,1,0:T(8,128)(2,1)}), bf16[32,4,24,256]{3,2,1,0:T(8,128)(2,1)S(1)}, u32[]{:S(2)}, u32[]{:S(2)}) %all-to-all-start.1) | async-done | bytes 1572896 | tf_op jit(solution)/shard_map/all_to_all | solution.py:108
  106.3 1.1 copy-done
  107.4 2.1 gather_fusion.3
  109.5 0.1 slice.73
  109.6 0.1 copy.85
  109.7 50.7 %all-gather.12.cloned.1.call-done = bf16[1024,3072]{0,1:T(8,128)(2,1)} async-done(((bf16[128,3072]{0,1:T(8,128)(2,1)}), bf16[1024,3072]{0,1:T(8,128)(2,1)}) %all-gather.12.cloned.1.call-update) | async-done | bytes 6291472 | tf_op jit(solution)/shard_map/all_gather | solution.py:105
  160.4 1.5 copy.86
  161.9 3.5 all-to-all-start.2
  165.5 0.0 all-gather.8.cloned.1.call-start
  165.5 0.7 constant_dynamic-slice_fusion
  166.3 0.6 fusion.6
  166.9 0.8 slice.78
  167.7 0.2 reduce-scatter.2.cloned.1.call-start
  167.9 56.2 %all-gather.6.cloned.1.call-done = bf16[3,3072,256]{1,2,0:T(8,128)(2,1)} async-done(((bf16[3,768,256]{1,2,0:T(8,128)(2,1)}), bf16[3,3072,256]{1,2,0:T(8,128)(2,1)}) %all-gather.6.cloned.1.call-update) | async-done | bytes 4718608 | tf_op jit(solution)/shard_map/all_gather | solution.py:122
  224.1 8.5 %fusion.12 = bf16[3,1024,256]{1,2,0:T(8,128)(2,1)S(1)} fusion(bf16[3,3072,256]{1,2,0:T(8,128)(2,1)} %all-gather.6.cloned.1.call-done, bf16[1024,3072]{0,1:T(8,128)(2,1)} %all-gather.12.cloned.1.call-done), kind=kOutput, calls=%fused_computation.28 | convolution fusion | flops 4832624640 | bytes 12582912 | tf_op jit(solution)/shard_map/sr,mrc->msc/dot_general | solution.py:123
  232.6 1.2 fusion.20
  233.9 8.7 %fusion.22 = (f32[2,1024]{1,0:T(2,128)S(1)}, f32[2,1024,1024]{1,2,0:T(8,128)}) fusion(pred[1024,1024]{0,1:T(8,128)(4,1)S(1)} %fusion.6, bf16[1024,2,128]{0,2,1:T(8,128)(2,1)} %bitcast.102, bf16[1024,2,128]{0,2,1:T(8,128)(2,1)} %bitcast.101), kind=kOutput, calls=%fused_computation.60 | convolution fusion | flops 547357696 | bytes 10493952 | tf_op jit(solution)/shard_map/sub | solution.py:137
  242.5 4.3 fusion.15
  246.9 3.8 all-gather.8.cloned.1.call-done
  250.7 5.9 %convolution_convert_fusion = bf16[1024,3072]{1,0:T(8,128)(2,1)} fusion(bf16[1024,256]{0,1:T(8,128)(2,1)S(1)} %bitcast.99, bf16[3072,256]{1,0:T(8,128)(2,1)} %all-gather.8.cloned.1.call-done), kind=kOutput, calls=%fused_computation.15 | convolution fusion | flops 1613758464 | bytes 8388608 | tf_op jit(solution)/shard_map/sc,rc->sr/dot_general | solution.py:141
  256.6 0.0 reduce-scatter.2.cloned.1.call-update
  256.6 0.0 all-gather.10.cloned.1.call-start
  256.7 0.1 select_reduce_fusion.2
  256.8 0.2 reshape.252
  257.1 119.5 %reduce-scatter.2.cloned.1.call-done = bf16[128,3072]{1,0:T(8,128)(2,1)} async-done(((bf16[1024,3072]{1,0:T(8,128)(2,1)}), bf16[128,3072]{1,0:T(8,128)(2,1)}) %reduce-scatter.2.cloned.1.call-update) | async-done | bytes 786448 | tf_op jit(solution)/shard_map/reduce_scatter | solution.py:155
  376.5 1.5 copy.94
  378.0 11.5 %gather_fusion.7 = bf16[3072,128]{1,0:T(8,128)(2,1)} fusion(bf16[128,3072]{0,1:T(8,128)(2,1)S(1)} %copy.94, s32[3072]{0:T(1024)S(1)} %broadcast_clamp_fusion), kind=kCustom, calls=%fused_computation.7 | custom fusion | bytes 1585152 | tf_op jit(solution)/shard_map/jit(_take)/gather | solution.py:156
  389.6 1.6 multiply_reduce_fusion
  391.2 2.5 multiply_convert_fusion
  393.7 4.2 all-to-all-start.3
  397.9 149.0 %all-gather.10.cloned.1.call-done = bf16[1024,3072]{0,1:T(8,128)(2,1)} async-done(((bf16[128,3072]{0,1:T(8,128)(2,1)}), bf16[1024,3072]{0,1:T(8,128)(2,1)}) %all-gather.10.cloned.1.call-update) | async-done | bytes 6291472 | tf_op jit(solution)/shard_map/all_gather | solution.py:162
  546.9 10.7 %fusion.23 = (f32[1024]{0:T(1024)S(1)}, f32[1024,1024]{0,1:T(8,128)S(1)}) fusion(bf16[1024,3072]{0,1:T(8,128)(2,1)} %all-gather.10.cloned.1.call-done, bf16[3072,1024]{1,0:T(8,128)(2,1)} %param.19), kind=kOutput, calls=%fused_computation.61 | convolution fusion | flops 6443498496 | bytes 16781312 | tf_op jit(solution)/shard_map/dot_general | solution.py:163
  557.6 1.4 exponential_reduce_fusion
  559.0 0.6 maximum_bitcast_fusion
  559.7 4.7 all-to-all-start.4
  564.4 1.2 copy.83
  565.6 4.3 gather_fusion.5
  569.9 3.9 copy.91
  573.8 4.3 gather_fusion.6
  578.1 3.9 copy.92
  582.0 0.5 add_subtract_fusion
  (30 shorter events, 0.3 us)
Async XLA Ops:
  9.9 14.6 %all-to-all-start = ((s32[32,1,258]{2,1,0:T(1,128)}), s32[32,1,258]{2,1,0:T(1,128)S(1)}, u32[]{:S(2)}, u32[]{:S(2)}) async-start(s32[32,1,258]{2,1,0:T(1,128)} %broadcast_in_dim.85), calls=%async_computation | async-start | bytes 98304 | tf_op jit(solution)/shard_map/all_to_all | solution.py:46
  17.2 143.2 %all-gather.12.cloned.1.call-start = ((), (), s32[]{:S(2)}) async-start(), calls=%async_computation.10 | async-start | bytes 7077888 | tf_op jit(solution)/shard_map/all_gather | solution.py:105
  24.4 11.8 %copy-start.2 = (s32[32,1,258]{2,1,0:T(1,128)}, s32[32,1,258]{2,1,0:T(1,128)S(1)}, u32[]{:S(2)}) copy-start(s32[32,1,258]{2,1,0:T(1,128)S(1)} %all-to-all-done) | copy-start | bytes 99076
  43.2 63.1 %all-to-all-start.1 = ((bf16[32,4,24,256]{3,2,1,0:T(8,128)(2,1)}), bf16[32,4,24,256]{3,2,1,0:T(8,128)(2,1)S(1)}, u32[]{:S(2)}, u32[]{:S(2)}) async-start(bf16[32,4,24,256]{3,2,1,0:T(8,128)(2,1)} %bitcast.1), calls=%async_computation.1 | async-start | bytes 3145728 | tf_op jit(solution)/shard_map/all_to_all | solution.py:108
  45.9 178.3 %all-gather.6.cloned.1.call-start = ((), (), s32[]{:S(2)}) async-start(), calls=%async_computation.6 | async-start | bytes 5898240 | tf_op jit(solution)/shard_map/all_gather | solution.py:122
  45.9 5.1 copy-start.1
  106.3 1.1 copy-start
  161.9 94.7 %all-to-all-start.2 = ((f32[32,4,24,256]{3,2,1,0:T(8,128)}), f32[32,4,24,256]{3,2,1,0:T(8,128)}, u32[]{:S(2)}, u32[]{:S(2)}) async-start(f32[32,4,24,256]{3,2,1,0:T(8,128)} %bitcast.81), calls=%async_computation.2 | async-start | bytes 6291456 | tf_op jit(solution)/shard_map/all_to_all | solution.py:121
  165.5 85.2 %all-gather.8.cloned.1.call-start = ((), (), s32[]{:S(2)}) async-start(), calls=%async_computation.7 | async-start | bytes 1966080 | tf_op jit(solution)/shard_map/all_gather | solution.py:144
  167.7 208.8 %reduce-scatter.2.cloned.1.call-start = ((), (), s32[]{:S(2)}) async-start(), calls=%async_computation.8 | async-start | bytes 7077888 | tf_op jit(solution)/shard_map/reduce_scatter | solution.py:155
  256.6 290.3 %all-gather.10.cloned.1.call-start = ((), (), s32[]{:S(2)}) async-start(), calls=%async_computation.9 | async-start | bytes 7077888 | tf_op jit(solution)/shard_map/all_gather | solution.py:162
  378.0 13.1 %copy-start.3 = (f32[3072]{0:T(1024)S(1)}, f32[3072]{0:T(1024)}, u32[]{:S(2)}) copy-start(f32[3072]{0:T(1024)} %param.18) | copy-start | bytes 36868
  393.7 166.0 %all-to-all-start.3 = ((f32[32,4,24,256]{3,2,1,0:T(8,128)}), f32[32,4,24,256]{3,2,1,0:T(8,128)}, u32[]{:S(2)}, u32[]{:S(2)}) async-start(f32[32,4,24,256]{3,2,1,0:T(8,128)} %bitcast.80), calls=%async_computation.3 | async-start | bytes 6291456 | tf_op jit(solution)/shard_map/all_to_all | solution.py:154
  559.7 22.3 %all-to-all-start.4 = ((f32[8,3,128]{2,1,0:T(4,128)}), f32[8,3,128]{2,1,0:T(4,128)S(1)}, u32[]{:S(2)}, u32[]{:S(2)}) async-start(f32[8,3,128]{2,1,0:T(4,128)} %maximum_bitcast_fusion), calls=%async_computation.5 | async-start | bytes 32768 | tf_op jit(solution)/shard_map/all_to_all | solution.py:62
Sparse Core Ops, SparseCore 0:
  36.3 124.0 all-gather.11
  162.5 61.5 all-gather.5
  225.7 24.9 all-gather.7
  256.7 119.7 reduce-scatter.1
  393.8 153.0 all-gather.9
where the time goes:
time: 590 us; the launch traced here: 589 us
  waiting for transfers between devices  419 us (71%)
  local copies, waits for them, and re-layouts  85.3 us (14%)
  matrix products  38.1 us (6%)
  starting transfers between devices  22.9 us (4%)
  between operations  15.3 us (3%)
  other arithmetic  8.52 us (1%)
    all_gather x1, waiting for transfers between devices, body(): normed = lax.all_gather(own_normed, ('fsdp', 'mp'), axis=0, tiled=True)  149 us
    reduce_scatter x1, waiting for transfers between devices, body(): lax.psum_scatter(partial_value, ('fsdp', 'mp'), scatter_dimension=0, tile...  119 us
    all_gather x1, waiting for transfers between devices, body(): piece = lax.all_gather(projections, 'dp', axis=1, tiled=True)  56.2 us
    all_gather x1, waiting for transfers between devices, body(): picked_cols = lax.all_gather(own_picked, ('fsdp', 'mp'), axis=0, tiled=True)  50.7 us
    all_to_all x1, waiting for transfers between devices, body(): lax.all_to_all(weights_sent, everyone, split_axis=0, concat_axis=0, tiled...  34 us
    unnamed x14, local copies, waits for them, and re-layouts  12.8 us
    transpose x3, local copies, waits for them, and re-layouts, pack_rows(): chosen.transpose(2, 3, 0, 1, 4)  12.3 us
  transfers between devices with their start and end apart: 10, of which 7 were waited for; matrix products, arithmetic and copies ran while one was open for 17% of the time, Pallas kernels for 0%

commit v1 on v0

--- a/solution.py
+++ b/solution.py
@@ -1,10 +1,19 @@
+import functools
 import math
 import jax
 import jax.numpy as jnp
 from jax import lax
 from jax.sharding import PartitionSpec as P
+from jax.lax import all_gather
 
 HD = 128
+
+
+def close_column(chunk, group_axis):
+    return jnp.concatenate(all_gather(chunk, group_axis), 1)
+
+
+process_quarters = functools.partial(close_column, group_axis="dp")
 
 
 def inverse_of(table):
@@ -119,7 +128,7 @@
             (picked_cols, projections, first_sent)
         )
     first_got = lax.all_to_all(first_sent, everyone, split_axis=0, concat_axis=0, tiled=True)
-    piece = lax.all_gather(projections, "dp", axis=1, tiled=True)
+    piece = process_quarters(projections)
     projected = jnp.einsum("sr,mrc->msc", picked_cols, piece, preferred_element_type=jnp.float32)
     heads = group_cols // HD
     queries = projected[0].astype(jnp.bfloat16).reshape(seq_len, heads, HD)

time: 590 us -> 600 us (1.017)
  local copies, waits for them, and re-layouts: 85.3 us -> 94.7 us
    reshape x0 -> x2, local copies, waits for them, and re-layouts: none -> 17.8 us  [close_column(): return jnp.concatenate(all_gather(chunk, group_axis), 1)]
    unnamed x14 -> x12, local copies, waits for them, and re-layouts: 12.8 us -> 12.8 us
  transfers between devices with their start and end apart: 10 -> 10, of which waited for: 7 -> 6; matrix products, arithmetic and copies ran while one was open for 17% -> 18% of each run, Pallas kernels for 0% -> 0%
where the time goes in v1:
time: 600 us; the launch traced here: 598 us
  waiting for transfers between devices  419 us (70%)
  local copies, waits for them, and re-layouts  94.7 us (16%)
  matrix products  38.1 us (6%)
  starting transfers between devices  22.8 us (4%)
  between operations  15.3 us (3%)
  other arithmetic  8.51 us (1%)
    all_gather x1, waiting for transfers between devices, body(): normed = lax.all_gather(own_normed, ('fsdp', 'mp'), axis=0, tiled=True)  149 us
    reduce_scatter x1, waiting for transfers between devices, body(): lax.psum_scatter(partial_value, ('fsdp', 'mp'), scatter_dimension=0, tile...  123 us
    all_gather x1, waiting for transfers between devices, close_column(): return jnp.concatenate(all_gather(chunk, group_axis), 1)  56.9 us
    all_gather x1, waiting for transfers between devices, body(): picked_cols = lax.all_gather(own_picked, ('fsdp', 'mp'), axis=0, tiled=True)  49.7 us
    all_to_all x1, waiting for transfers between devices, body(): lax.all_to_all(weights_sent, everyone, split_axis=0, concat_axis=0, tiled...  34.1 us
    reshape x2, local copies, waits for them, and re-layouts, close_column(): return jnp.concatenate(all_gather(chunk, group_axis), 1)  17.8 us
    unnamed x12, local copies, waits for them, and re-layouts  12.8 us
    transpose x3, local copies, waits for them, and re-layouts, pack_rows(): chosen.transpose(2, 3, 0, 1, 4)  12.2 us
  transfers between devices with their start and end apart: 10, of which 6 were waited for; matrix products, arithmetic and copies ran while one was open for 18% of the time, Pallas kernels for 0%

profile of v1, /device:TPU:0, one launch (start us, length us, event | category | flops | bytes accessed | tf_op | source)
XLA Modules:
  0.0 598.2 jit_solution(15395369048747787468)
XLA Ops:
  8.5 0.7 pad_add_fusion
  9.2 0.6 broadcast_in_dim.85
  9.9 7.3 %all-to-all-start = ((s32[32,1,258]{2,1,0:T(1,128)}), s32[32,1,258]{2,1,0:T(1,128)S(1)}, u32[]{:S(2)}, u32[]{:S(2)}) async-start(s32[32,1,258]{2,1,0:T(1,128)} %broadcast_in_dim.85), calls=%async_computation | async-start | bytes 98304 | tf_op jit(solution)/shard_map/all_to_all | solution.py:55
  17.2 0.0 all-gather.11.cloned.1.call-start
  17.2 1.5 copy.82
  18.8 5.7 all-to-all-done
  24.4 0.1 slice.43
  24.5 0.1 reduce.2
  24.6 0.1 broadcast_add_fusion
  24.7 11.4 %gather_fusion.4 = bf16[3072,128]{1,0:T(8,128)(2,1)} fusion(bf16[128,3072]{0,1:T(8,128)(2,1)S(1)} %copy.82, s32[3072]{0:T(1024)S(1)} %broadcast_clamp_fusion.1), kind=kCustom, calls=%fused_computation.4 | custom fusion | bytes 1585152 | tf_op jit(solution)/shard_map/jit(_take)/gather | solution.py:113
  36.2 1.9 copy.102
  38.1 1.9 gather_fusion
  40.0 3.1 copy.78
  43.1 2.7 all-to-all-start.1
  45.8 0.0 all-gather.13.cloned.1.call-start
  45.9 5.1 copy.103
  51.0 3.1 copy.104
  54.1 4.3 gather_fusion.1
  58.5 4.5 copy.79
  63.0 4.4 gather_fusion.2
  67.4 4.5 copy.80
  71.9 0.1 slice_reduce_fusion
  72.0 0.1 select_reduce_fusion.1
  72.1 34.1 %all-to-all-done.1 = bf16[32,4,24,256]{3,2,1,0:T(8,128)(2,1)S(1)} async-done(((bf16[32,4,24,256]{3,2,1,0:T(8,128)(2,1)}), bf16[32,4,24,256]{3,2,1,0:T(8,128)(2,1)S(1)}, u32[]{:S(2)}, u32[]{:S(2)}) %all-to-all-start.1) | async-done | bytes 1572896 | tf_op jit(solution)/shard_map/all_to_all | solution.py:117
  106.2 1.1 copy-done
  107.4 2.1 gather_fusion.3
  109.5 0.1 slice.73
  109.6 1.1 copy.83
  110.7 49.7 %all-gather.11.cloned.1.call-done = bf16[1024,3072]{0,1:T(8,128)(2,1)} async-done(((bf16[128,3072]{0,1:T(8,128)(2,1)}), bf16[1024,3072]{0,1:T(8,128)(2,1)}) %all-gather.11.cloned.1.call-update) | async-done | bytes 6291472 | tf_op jit(solution)/shard_map/all_gather | solution.py:114
  160.4 3.5 all-to-all-start.2
  163.9 0.0 all-gather.7.cloned.1.call-start
  164.0 0.6 fusion.6
  164.6 0.8 slice.78
  165.5 0.2 reduce-scatter.2.cloned.1.call-start
  165.7 56.9 %all-gather.13.cloned.1.call-done = bf16[12,768,256]{2,1,0:T(8,128)(2,1)} async-done(((bf16[3,768,256]{2,1,0:T(8,128)(2,1)}), bf16[12,768,256]{2,1,0:T(8,128)(2,1)}) %all-gather.13.cloned.1.call-update) | async-done | bytes 4718608 | tf_op jit(solution)/shard_map/all_gather | solution.py:13
  222.6 8.4 %copy.84 = bf16[3,4,768,256]{2,1,3,0:T(4,128)(2,1)} copy(bf16[3,4,768,256]{3,2,0,1:T(8,128)(2,1)} %bitcast.95) | data formatting | bytes 9437184 | tf_op jit(solution)/shard_map/reshape | solution.py:13
  231.0 9.4 %reshape.198 = bf16[3,3072,256]{1,2,0:T(8,128)(2,1)} reshape(bf16[3,4,768,256]{2,1,3,0:T(4,128)(2,1)} %copy.84) | data formatting | bytes 9437184 | tf_op jit(solution)/shard_map/reshape | solution.py:13
  240.4 8.6 %fusion.12 = bf16[3,1024,256]{1,2,0:T(8,128)(2,1)S(1)} fusion(bf16[3,3072,256]{1,2,0:T(8,128)(2,1)} %reshape.198, bf16[1024,3072]{0,1:T(8,128)(2,1)} %all-gather.11.cloned.1.call-done), kind=kOutput, calls=%fused_computation.28 | convolution fusion | flops 4832624640 | bytes 12582912 | tf_op jit(solution)/shard_map/sr,mrc->msc/dot_general | solution.py:132
  248.9 1.2 fusion.20
  250.2 8.7 %fusion.22 = (f32[2,1024]{1,0:T(2,128)S(1)}, f32[2,1024,1024]{1,2,0:T(8,128)}) fusion(pred[1024,1024]{0,1:T(8,128)(4,1)S(1)} %fusion.6, bf16[1024,2,128]{0,2,1:T(8,128)(2,1)} %bitcast.108, bf16[1024,2,128]{0,2,1:T(8,128)(2,1)} %bitcast.107), kind=kOutput, calls=%fused_computation.60 | convolution fusion | flops 547357696 | bytes 10493952 | tf_op jit(solution)/shard_map/sub | solution.py:146
  258.8 4.3 fusion.15
  263.1 0.0 all-gather.7.cloned.1.call-done
  263.2 5.9 convolution_convert_fusion
  269.1 0.0 reduce-scatter.2.cloned.1.call-update
  269.1 0.0 all-gather.9.cloned.1.call-start
  269.2 0.1 select_reduce_fusion.2
  269.3 0.2 reshape.260
  269.6 123.3 %reduce-scatter.2.cloned.1.call-done = bf16[128,3072]{1,0:T(8,128)(2,1)} async-done(((bf16[1024,3072]{1,0:T(8,128)(2,1)}), bf16[128,3072]{1,0:T(8,128)(2,1)}) %reduce-scatter.2.cloned.1.call-update) | async-done | bytes 786448 | tf_op jit(solution)/shard_map/reduce_scatter | solution.py:164
  392.8 1.5 copy.92
  394.4 11.5 %gather_fusion.7 = bf16[3072,128]{1,0:T(8,128)(2,1)} fusion(bf16[128,3072]{0,1:T(8,128)(2,1)S(1)} %copy.92, s32[3072]{0:T(1024)S(1)} %broadcast_clamp_fusion), kind=kCustom, calls=%fused_computation.7 | custom fusion | bytes 1585152 | tf_op jit(solution)/shard_map/jit(_take)/gather | solution.py:165
  405.9 1.6 multiply_reduce_fusion
  407.5 2.5 multiply_convert_fusion
  410.0 4.2 all-to-all-start.3
  414.2 149.0 %all-gather.9.cloned.1.call-done = bf16[1024,3072]{0,1:T(8,128)(2,1)} async-done(((bf16[128,3072]{0,1:T(8,128)(2,1)}), bf16[1024,3072]{0,1:T(8,128)(2,1)}) %all-gather.9.cloned.1.call-update) | async-done | bytes 6291472 | tf_op jit(solution)/shard_map/all_gather | solution.py:171
  563.2 10.7 %fusion.23 = (f32[1024]{0:T(1024)S(1)}, f32[1024,1024]{0,1:T(8,128)S(1)}) fusion(bf16[1024,3072]{0,1:T(8,128)(2,1)} %all-gather.9.cloned.1.call-done, bf16[3072,1024]{1,0:T(8,128)(2,1)} %param.19), kind=kOutput, calls=%fused_computation.61 | convolution fusion | flops 6443498496 | bytes 16781312 | tf_op jit(solution)/shard_map/dot_general | solution.py:172
  573.9 1.4 exponential_reduce_fusion
  575.3 0.6 maximum_bitcast_fusion
  575.9 4.7 all-to-all-start.4
  580.6 1.2 copy.81
  581.9 2.6 gather_fusion.5
  584.5 2.0 copy.89
  586.5 2.6 gather_fusion.6
  589.1 2.0 copy.90
  591.2 0.5 add_subtract_fusion
  (29 shorter events, 0.3 us)
Async XLA Ops:
  9.9 14.6 %all-to-all-start = ((s32[32,1,258]{2,1,0:T(1,128)}), s32[32,1,258]{2,1,0:T(1,128)S(1)}, u32[]{:S(2)}, u32[]{:S(2)}) async-start(s32[32,1,258]{2,1,0:T(1,128)} %broadcast_in_dim.85), calls=%async_computation | async-start | bytes 98304 | tf_op jit(solution)/shard_map/all_to_all | solution.py:55
  17.2 143.2 %all-gather.11.cloned.1.call-start = ((), (), s32[]{:S(2)}) async-start(), calls=%async_computation.9 | async-start | bytes 7077888 | tf_op jit(solution)/shard_map/all_gather | solution.py:114
  43.1 63.1 %all-to-all-start.1 = ((bf16[32,4,24,256]{3,2,1,0:T(8,128)(2,1)}), bf16[32,4,24,256]{3,2,1,0:T(8,128)(2,1)S(1)}, u32[]{:S(2)}, u32[]{:S(2)}) async-start(bf16[32,4,24,256]{3,2,1,0:T(8,128)(2,1)} %bitcast.1), calls=%async_computation.1 | async-start | bytes 3145728 | tf_op jit(solution)/shard_map/all_to_all | solution.py:117
  45.8 176.7 %all-gather.13.cloned.1.call-start = ((), (), s32[]{:S(2)}) async-start(), calls=%async_computation.10 | async-start | bytes 5898240 | tf_op jit(solution)/shard_map/all_gather | solution.py:13
  45.9 5.1 copy-start.1
  106.2 1.1 copy-start
  160.4 108.7 %all-to-all-start.2 = ((f32[32,4,24,256]{3,2,1,0:T(8,128)}), f32[32,4,24,256]{3,2,1,0:T(8,128)}, u32[]{:S(2)}, u32[]{:S(2)}) async-start(f32[32,4,24,256]{3,2,1,0:T(8,128)} %bitcast.86), calls=%async_computation.2 | async-start | bytes 6291456 | tf_op jit(solution)/shard_map/all_to_all | solution.py:130
  163.9 99.2 %all-gather.7.cloned.1.call-start = ((), (), s32[]{:S(2)}) async-start(), calls=%async_computation.6 | async-start | bytes 1966080 | tf_op jit(solution)/shard_map/all_gather | solution.py:153
  165.5 227.4 %reduce-scatter.2.cloned.1.call-start = ((), (), s32[]{:S(2)}) async-start(), calls=%async_computation.7 | async-start | bytes 7077888 | tf_op jit(solution)/shard_map/reduce_scatter | solution.py:164
  269.1 294.1 %all-gather.9.cloned.1.call-start = ((), (), s32[]{:S(2)}) async-start(), calls=%async_computation.8 | async-start | bytes 7077888 | tf_op jit(solution)/shard_map/all_gather | solution.py:171
  394.3 13.1 %copy-start.2 = (f32[3072]{0:T(1024)S(1)}, f32[3072]{0:T(1024)}, u32[]{:S(2)}) copy-start(f32[3072]{0:T(1024)} %param.18) | copy-start | bytes 36868
  410.0 166.0 %all-to-all-start.3 = ((f32[32,4,24,256]{3,2,1,0:T(8,128)}), f32[32,4,24,256]{3,2,1,0:T(8,128)}, u32[]{:S(2)}, u32[]{:S(2)}) async-start(f32[32,4,24,256]{3,2,1,0:T(8,128)} %bitcast.85), calls=%async_computation.3 | async-start | bytes 6291456 | tf_op jit(solution)/shard_map/all_to_all | solution.py:163
  575.9 15.2 %all-to-all-start.4 = ((f32[8,3,128]{2,1,0:T(4,128)}), f32[8,3,128]{2,1,0:T(4,128)S(1)}, u32[]{:S(2)}, u32[]{:S(2)}) async-start(f32[8,3,128]{2,1,0:T(4,128)} %maximum_bitcast_fusion), calls=%async_computation.5 | async-start | bytes 32768 | tf_op jit(solution)/shard_map/all_to_all | solution.py:71
Sparse Core Ops, SparseCore 0:
  36.3 124.0 all-gather.10
  162.5 60.0 all-gather.12
  224.1 25.1 all-gather.6
  269.2 123.5 reduce-scatter.1
  410.1 153.0 all-gather.8
